TPU v7x, 32 devices: a whole 2x2x4 slice. The times are simulated.
32 devices in a mesh: gx: 2 (over x), gy: 4 (over y, core), gz: 4 (over z).
Axes of the slice: x: 2, y: 2, z: 4, core: 2. Of those that a mesh axis runs over, the one named last changes fastest.
Arguments:
- vorticity: float32 [3, 16, 64, 512], P(None, 'gx', 'gy', 'gz'), may hold values from -6 to 6
- velocity: float32 [3, 16, 64, 512], P(None, 'gx', 'gy', 'gz'), may hold values from -1 to 1
Outputs:
- vorticity_out: float32 [3, 16, 64, 512], P(None, 'gx', 'gy', 'gz')
All inputs are finite; a program needn't handle non-finite values.
Results may differ from a plain program's by a relative error of at most 0.0003.
Values sent between devices are 32-bit elements; how exact they have to be, the bound alone decides.
A program may use at most 64 MiB of HBM per device.

v0:
```python
import functools

import jax
import jax.numpy as jnp
from jax import lax
from jax.experimental import pallas as pl
from jax.experimental.pallas import tpu as pltpu
from jax.sharding import PartitionSpec as P

SUBSTEPS = 2
TIME_STEP = 0.5
AXES = ("gx", "gy", "gz")
MESH = pl.DeviceIdType.MESH


def roll(values, shift, axis):
    return pltpu.roll(values, shift % values.shape[axis], axis)


def weights(velocity):
    d = TIME_STEP * velocity
    s = jnp.abs(d)
    t = 1.0 - s
    positive = d > 0.0
    centre = 1.0 + s * s * (1.5 * s - 2.5)
    toward = 1.0 + t * t * (1.5 * t - 2.5)
    away = -0.5 * s * t * t
    beyond = -0.5 * s * s * t
    return (
        jnp.where(positive, 0.0, beyond),
        jnp.where(positive, away, toward),
        centre,
        jnp.where(positive, toward, away),
        jnp.where(positive, beyond, 0.0),
    )


def body(
    sizes, vort, vel, out, wgt, slope, cur, sx, rx, sy, ry, sz, rz, rvx, svy, rvy, svz, rvz,
    send_sem, recv_sem,
):
    _, X, Y, Z = vort.shape
    here = [lax.axis_index(a) for a in AXES]

    def neighbour(k, side):
        n = sizes[k]
        moved = lax.rem(here[k] + (1 if side else n - 1), n)
        return tuple(moved if j == k else here[j] for j in range(3))

    def push(src, dst, index, k, side):
        copy = pltpu.make_async_remote_copy(
            src_ref=src, dst_ref=dst, send_sem=send_sem.at[index], recv_sem=recv_sem.at[index],
            device_id=neighbour(k, side), device_id_type=MESH,
        )
        copy.start()
        return copy

    barrier = pltpu.get_barrier_semaphore()
    for k in range(3):
        for side in range(2):
            pl.semaphore_signal(barrier, inc=1, device_id=neighbour(k, side), device_id_type=MESH)

    lane = lax.broadcasted_iota(jnp.int32, (8, Z), 1)
    lane3 = lax.broadcasted_iota(jnp.int32, (X, Y, Z), 2)
    row3 = lax.broadcasted_iota(jnp.int32, (X, Y, Z), 1)
    slabs = [(c, x, y) for c in range(3) for x in range(X) for y in range(0, Y, 8)]
    per = Z // 4

    def pack(edges, target):
        for m in range(0, len(slabs), per):
            held = jnp.zeros((8, Z), jnp.float32)
            for k, (c, x, y) in enumerate(slabs[m:m + per]):
                moved = roll(edges[c][x, y:y + 8, :], 4 * k + 2, 1)
                held = jnp.where(lane // 4 == k, moved, held)
            target[m // per] = held

    def unpack(low_side, high_side):
        merged = [
            jnp.where(lane % 4 >= 2, low_side[m], high_side[m])
            for m in range(-(-len(slabs) // per))
        ]
        edge = (lane < 2) | (lane >= Z - 2)
        return [
            jnp.where(edge, roll(merged[i // per], -(4 * (i % per) + 2), 1), 0.0)
            for i in range(len(slabs))
        ]

    def spread_x(src, step):
        for c in range(3):
            w = [wgt.at[0, a] for a in range(5)]
            sx[step, 0, c, 0] = w[0][0] * src[c, 0]
            sx[step, 0, c, 1] = w[1][0] * src[c, 0] + w[0][1] * src[c, 1]
            sx[step, 1, c, 0] = w[3][X - 1] * src[c, X - 1] + w[4][X - 2] * src[c, X - 2]
            sx[step, 1, c, 1] = w[4][X - 1] * src[c, X - 1]

    def interior_x(src):
        for c in range(3):
            layers = []
            for x in range(X):
                total = None
                for a in range(-2, 3):
                    if 0 <= x - a < X:
                        term = wgt[0, a + 2, x - a] * src[c, x - a]
                        total = term if total is None else total + term
                layers.append(total)
            for x in range(X):
                yield c, x, layers[x]

    def put_weights(k):
        for a, w in enumerate(weights(vel[k])):
            wgt[k, a] = w

    put_weights(0)
    spread_x(vort, 0)
    pl.semaphore_wait(barrier, 6)
    pending = []
    first = [push(sx.at[0, s], rx.at[0, s], s, 0, s) for s in range(2)]
    for s in range(2):
        svy[s] = vel[:, :, pl.ds((Y - 2) * s, 2), :]
    pack([vel[c] for c in range(3)], svz)
    vy = [push(svy.at[s], rvy.at[s], 14 + s, 1, s) for s in range(2)]
    vz = [push(svz, rvz.at[s], 16 + s, 2, s) for s in range(2)]
    vx = [push(vel.at[:, pl.ds((X - 2) * s, 2)], rvx.at[s], 12 + s, 0, s) for s in range(2)]
    put_weights(1)
    put_weights(2)

    scale = TIME_STEP / 12.0

    def slopes_y():
        for c in range(3):
            v = vel[c]
            near = 8.0 * (roll(v, -1, 1) - roll(v, 1, 1)) - (roll(v, -2, 1) - roll(v, 2, 1))
            slope[1, c] = near * scale
        for cp in vy:
            cp.wait()
        for c in range(3):
            top = vel[c, :, 0:4, :]
            low = rvy[1, c]
            slope[1, c, :, 0:1, :] = scale * (
                8.0 * (top[:, 1:2] - low[:, 1:2]) - (top[:, 2:3] - low[:, 0:1]))
            slope[1, c, :, 1:2, :] = scale * (
                8.0 * (top[:, 2:3] - top[:, 0:1]) - (top[:, 3:4] - low[:, 1:2]))
            end = vel[c, :, Y - 4:Y, :]
            high = rvy[0, c]
            slope[1, c, :, Y - 2:Y - 1, :] = scale * (
                8.0 * (end[:, 3:4] - end[:, 1:2]) - (high[:, 0:1] - end[:, 0:1]))
            slope[1, c, :, Y - 1:Y, :] = scale * (
                8.0 * (high[:, 0:1] - end[:, 2:3]) - (high[:, 1:2] - end[:, 1:2]))

    def slopes_z():
        for cp in vz:
            cp.wait()
        halo = unpack(rvz.at[0], rvz.at[1])
        for i, (c, x, y) in enumerate(slabs):
            v = vel[c, x, y:y + 8, :]
            h = halo[i]

            def at(shift):
                source = roll(v, -shift, 1)
                if shift > 0:
                    return jnp.where(lane >= Z - shift, roll(h, -shift, 1), source)
                return jnp.where(lane < -shift, roll(h, -shift, 1), source)

            slope[2, c, x, y:y + 8, :] = scale * (8.0 * (at(1) - at(-1)) - (at(2) - at(-2)))

    def slopes_x():
        for cp in vx:
            cp.wait()
        for c in range(3):
            def layer(x):
                if x < 0:
                    return rvx[1, c, x + 2]
                if x >= X:
                    return rvx[0, c, x - X]
                return vel[c, x]
            for x in range(X):
                slope[0, c, x] = scale * (
                    8.0 * (layer(x + 1) - layer(x - 1)) - (layer(x + 2) - layer(x - 2)))

    for step in range(SUBSTEPS):
        base = step * 6
        src = vort if step == 0 else cur
        if step > 0:
            spread_x(src, step)
            first = [push(sx.at[step, s], rx.at[step, s], base + s, 0, s) for s in range(2)]
        for c, x, layer in interior_x(src):
            cur[c, x] = layer
        if step == 0:
            slopes_y()
            slopes_z()
        for cp in first:
            cp.wait()
        for c in range(3):
            for x in range(2):
                cur[c, x] += rx[step, 1, c, x]
                cur[c, X - 2 + x] += rx[step, 0, c, x]

        for c in range(3):
            v = cur[c]
            u = [wgt[1, a] * v for a in range(5)]
            keep, go = u[2], None
            for a in (-2, -1, 1, 2):
                moved = roll(u[a + 2], a, 1)
                outside = row3 < a if a > 0 else row3 >= Y + a
                keep = keep + jnp.where(outside, 0.0, moved)
                part = jnp.where(outside, moved, 0.0)
                go = part if go is None else go + part
            cur[c] = keep
            sy[step, 1, c] = go[:, 0:2, :]
            sy[step, 0, c] = go[:, Y - 2:Y, :]
        copies = [push(sy.at[step, s], ry.at[step, s], base + 2 + s, 1, s) for s in range(2)]
        if step == 0:
            slopes_x()
        for cp in copies:
            cp.wait()
        for c in range(3):
            cur[c, :, 0:2, :] += ry[step, 1, c]
            cur[c, :, Y - 2:Y, :] += ry[step, 0, c]

        edges = []
        for c in range(3):
            v = cur[c]
            u = [wgt[2, a] * v for a in range(5)]
            keep, go = u[2], None
            for a in (-2, -1, 1, 2):
                moved = roll(u[a + 2], a, 2)
                outside = lane3 < a if a > 0 else lane3 >= Z + a
                keep = keep + jnp.where(outside, 0.0, moved)
                part = jnp.where(outside, moved, 0.0)
                go = part if go is None else go + part
            cur[c] = keep
            edges.append(go)
        pack(edges, sz.at[step])
        copies = [push(sz.at[step], rz.at[step, s], base + 4 + s, 2, s) for s in range(2)]
        for cp in copies:
            cp.wait()
        halo = unpack(rz.at[step, 1], rz.at[step, 0])
        final = out if step == SUBSTEPS - 1 else cur
        for x in range(X):
            for y in range(0, Y, 8):
                v = [
                    cur[c, x, y:y + 8, :] + halo[slabs.index((c, x, y))]
                    for c in range(3)
                ]
                for i in range(3):
                    total = v[i]
                    for j in range(3):
                        total = total + v[j] * slope[j, i, x, y:y + 8, :]
                    final[i, x, y:y + 8, :] = total


def solution(mesh):
    sizes = [mesh.shape[a] for a in AXES]

    def local(vort, vel):
        _, X, Y, Z = vort.shape
        packs = -(-(3 * X * (Y // 8)) // (Z // 4))
        f32 = jnp.float32
        V = pltpu.VMEM
        S = SUBSTEPS
        return pl.pallas_call(
            functools.partial(body, sizes),
            out_shape=jax.ShapeDtypeStruct(vort.shape, f32),
            in_specs=[pl.BlockSpec(memory_space=pltpu.VMEM)] * 2,
            out_specs=pl.BlockSpec(memory_space=pltpu.VMEM),
            scratch_shapes=[
                V((3, 5, X, Y, Z), f32),
                V((3, 3, X, Y, Z), f32),
                V((3, X, Y, Z), f32),
                V((S, 2, 3, 2, Y, Z), f32),
                V((S, 2, 3, 2, Y, Z), f32),
                V((S, 2, 3, X, 2, Z), f32),
                V((S, 2, 3, X, 2, Z), f32),
                V((S, packs, 8, Z), f32),
                V((S, 2, packs, 8, Z), f32),
                V((2, 3, 2, Y, Z), f32),
                V((2, 3, X, 2, Z), f32),
                V((2, 3, X, 2, Z), f32),
                V((packs, 8, Z), f32),
                V((2, packs, 8, Z), f32),
                pltpu.SemaphoreType.DMA((18,)),
                pltpu.SemaphoreType.DMA((18,)),
            ],
            compiler_params=pltpu.CompilerParams(collective_id=0, has_side_effects=True),
        )(vort, vel)

    placed = P(None, *AXES)
    return jax.shard_map(
        local, mesh=mesh, in_specs=(placed, placed), out_specs=placed, check_vma=False
    )
```

profile of v0, /device:TPU:0, one launch (start us, length us, event | category | flops | bytes accessed | tf_op | source)
XLA Modules:
  0.0 29.8 jit_solution(2979071157916114914)
XLA Ops:
  0.0 28.1 %shard_map.28 = f32[3,8,16,128]{3,2,1,0:T(8,128)} custom-call(f32[3,8,16,128]{3,2,1,0:T(8,128)} %vort.1, f32[3,8,16,128]{3,2,1,0:T(8,128)} %vel.1), custom_call_target="tpu_custom_call" | custom-call | tf_op jit(solution)/shard_map/pallas_call | solution.py:261
  28.1 1.6 %copy.4 = f32[3,8,16,128]{3,2,1,0:T(8,128)} copy(f32[3,8,16,128]{3,2,1,0:T(8,128)} %shard_map.28) | data formatting | bytes 393216
where the time goes:
time: 29.9 us; the launch traced here: 29.8 us
  Pallas kernels  28.1 us (94%)
  local copies, waits for them, and re-layouts  1.62 us (5%)
    pallas_call x1, Pallas kernels, local(): pl.pallas_call(functools.partial(body, sizes), out_shape=jax.ShapeDtypeSt...  28.1 us
    unnamed x1, local copies, waits for them, and re-layouts  1.62 us

commit v1 on v0

--- a/solution.py
+++ b/solution.py
@@ -36,8 +36,8 @@
 
 
 def body(
-    sizes, vort, vel, out, wgt, slope, cur, sx, rx, sy, ry, sz, rz, rvx, svy, rvy, svz, rvz,
-    send_sem, recv_sem,
+    sizes, vort_hbm, vel_hbm, out, vort, vel, wgt, slope, cur, sx, rx, sy, ry, sz, rz, rvx, svy, rvy, svz, rvz,
+    send_sem, recv_sem, load_sem,
 ):
     _, X, Y, Z = vort.shape
     here = [lax.axis_index(a) for a in AXES]
@@ -59,6 +59,13 @@
     for k in range(3):
         for side in range(2):
             pl.semaphore_signal(barrier, inc=1, device_id=neighbour(k, side), device_id_type=MESH)
+
+    loads = [
+        pltpu.make_async_copy(vel_hbm, vel, load_sem.at[0]),
+        pltpu.make_async_copy(vort_hbm, vort, load_sem.at[1]),
+    ]
+    for cp in loads:
+        cp.start()
 
     lane = lax.broadcasted_iota(jnp.int32, (8, Z), 1)
     lane3 = lax.broadcasted_iota(jnp.int32, (X, Y, Z), 2)
@@ -110,7 +117,9 @@
         for a, w in enumerate(weights(vel[k])):
             wgt[k, a] = w
 
+    loads[0].wait()
     put_weights(0)
+    loads[1].wait()
     spread_x(vort, 0)
     pl.semaphore_wait(barrier, 6)
     pending = []
@@ -260,10 +269,12 @@
         S = SUBSTEPS
         return pl.pallas_call(
             functools.partial(body, sizes),
-            out_shape=jax.ShapeDtypeStruct(vort.shape, f32),
-            in_specs=[pl.BlockSpec(memory_space=pltpu.VMEM)] * 2,
+            out_shape=V(vort.shape, f32),
+            in_specs=[pl.BlockSpec(memory_space=pl.ANY)] * 2,
             out_specs=pl.BlockSpec(memory_space=pltpu.VMEM),
             scratch_shapes=[
+                V(vort.shape, f32),
+                V(vort.shape, f32),
                 V((3, 5, X, Y, Z), f32),
                 V((3, 3, X, Y, Z), f32),
                 V((3, X, Y, Z), f32),
@@ -280,6 +291,7 @@
                 V((2, packs, 8, Z), f32),
                 pltpu.SemaphoreType.DMA((18,)),
                 pltpu.SemaphoreType.DMA((18,)),
+                pltpu.SemaphoreType.DMA((2,)),
             ],
             compiler_params=pltpu.CompilerParams(collective_id=0, has_side_effects=True),
         )(vort, vel)

time: 29.9 us -> 27.3 us (0.913)
  Pallas kernels: 28.1 us -> 26.5 us
  local copies, waits for them, and re-layouts: 1.62 us -> 0.68 us
    pallas_call x1, Pallas kernels: 28.1 us -> 26.5 us  [local(): pl.pallas_call(functools.partial(body, sizes), out_shape=V(vort.shape, f3...]
    unnamed x1, local copies, waits for them, and re-layouts: 1.62 us -> 0.68 us
where the time goes in v1:
time: 27.3 us; the launch traced here: 27.2 us
  Pallas kernels  26.5 us (97%)
  local copies, waits for them, and re-layouts  0.68 us (2%)
    pallas_call x1, Pallas kernels, local(): pl.pallas_call(functools.partial(body, sizes), out_shape=V(vort.shape, f3...  26.5 us
    unnamed x1, local copies, waits for them, and re-layouts  0.68 us

profile of v1, /device:TPU:0, one launch (start us, length us, event | category | flops | bytes accessed | tf_op | source)
XLA Modules:
  0.0 27.2 jit_solution(8226804978933199669)
XLA Ops:
  0.0 26.5 %shard_map.28 = f32[3,8,16,128]{3,2,1,0:T(8,128)S(1)} custom-call(f32[3,8,16,128]{3,2,1,0:T(8,128)} %vort_hbm.1, f32[3,8,16,128]{3,2,1,0:T(8,128)} %vel_hbm.1), custom_call_target="tpu_custom_call" | custom-call | tf_op jit(solution)/shard_map/pallas_call | solution.py:270
  26.5 0.7 %copy.4 = f32[3,8,16,128]{3,2,1,0:T(8,128)} copy(f32[3,8,16,128]{3,2,1,0:T(8,128)S(1)} %shard_map.28) | data formatting | bytes 393216

commit v2 on v1

v2 whole, which is shorter than its diff:
```python
import functools

import jax
import jax.numpy as jnp
from jax import lax
from jax.experimental import pallas as pl
from jax.experimental.pallas import tpu as pltpu
from jax.sharding import PartitionSpec as P

SUBSTEPS = 2
TIME_STEP = 0.5
AXES = ("gx", "gy", "gz")
MESH = pl.DeviceIdType.MESH
SIDES = (-1, 1)


def roll(values, shift, axis):
    shift %= values.shape[axis]
    return pltpu.roll(values, shift, axis) if shift else values


def weights(velocity):
    d = TIME_STEP * velocity
    s = jnp.abs(d)
    t = 1.0 - s
    positive = d > 0.0
    centre = 1.0 + s * s * (1.5 * s - 2.5)
    toward = 1.0 + t * t * (1.5 * t - 2.5)
    away = -0.5 * s * t * t
    beyond = -0.5 * s * s * t
    return (
        jnp.where(positive, 0.0, beyond),
        jnp.where(positive, away, toward),
        centre,
        jnp.where(positive, toward, away),
        jnp.where(positive, beyond, 0.0),
    )


def inside(w, a, index, extent):
    if a == 0:
        return w
    return jnp.where(index < extent - a if a > 0 else index >= -a, w, 0.0)


def body(
    sizes, vort_hbm, vel_hbm, out, vort, vel, wgt, wgt_y, slope, cur,
    qvort, qvel, qcur, qwgt, qwgt_y, qslope,
    sx, rx, sy, ry, sxy, rxy, rvx, svy, rvy, sz, rz,
    sxq, rxq, syq, ryq, sxyq, rxyq,
    send_sem, recv_sem, load_sem,
):
    _, X, Y, Z = vort.shape
    W = Z // X
    assert W * X == Z and W >= 16 and X >= 6 and Y >= 8
    scale = TIME_STEP / 12.0
    here = [lax.axis_index(a) for a in AXES]

    def device(*offset):
        return tuple(
            here[k] if not d else lax.rem(here[k] + (d % sizes[k]), sizes[k])
            for k, d in enumerate(offset)
        )

    pushed = []

    def push(src, dst, offset):
        index = len(pushed)
        copy = pltpu.make_async_remote_copy(
            src_ref=src, dst_ref=dst, send_sem=send_sem.at[index], recv_sem=recv_sem.at[index],
            device_id=device(*offset), device_id_type=MESH,
        )
        copy.start()
        pushed.append(copy)
        return copy

    def arrived(copies):
        for copy in copies:
            copy.wait_recv()

    plane = [(dx, dy, 0) for dx in (-1, 0, 1) for dy in (-1, 0, 1) if dx or dy]
    greeted = plane + [(0, 0, -1)]
    barrier = pltpu.get_barrier_semaphore()
    for offset in greeted:
        pl.semaphore_signal(barrier, inc=1, device_id=device(*offset), device_id_type=MESH)
    loads = [
        pltpu.make_async_copy(vel_hbm, vel, load_sem.at[0]),
        pltpu.make_async_copy(vort_hbm, vort, load_sem.at[1]),
    ]
    for cp in loads:
        cp.start()

    lane = lax.broadcasted_iota(jnp.int32, (Y, Z), 1)
    row = lax.broadcasted_iota(jnp.int32, (Y, Z), 0)
    cell = lane % W
    edge = (lane < 2) | (lane >= Z - 2)

    def strip(src, c):
        held = roll(src[c, 0], 4, 1)
        for x in range(1, X):
            held = jnp.where(lane >= W * x, roll(src[c, x], W * x + 4, 1), held)
        return held

    def spread_x(src, step):
        w = [wgt.at[0, a] for a in range(5)]
        for c in range(3):
            sx[step, 0, c, 0] = w[0][0] * src[c, 0]
            sx[step, 0, c, 1] = w[1][0] * src[c, 0] + w[0][1] * src[c, 1]
            sx[step, 1, c, 0] = w[3][X - 1] * src[c, X - 1] + w[4][X - 2] * src[c, X - 2]
            sx[step, 1, c, 1] = w[4][X - 1] * src[c, X - 1]
            for s in range(2):
                for t in range(2):
                    sxy[step, s, t, c] = sx[step, s, c, :, pl.ds((Y - 2) * t, 2), :]

    def push_x(step):
        copies = [push(sx.at[step, s], rx.at[step, s], (SIDES[s], 0, 0)) for s in range(2)]
        copies += [
            push(sxy.at[step, s, t], rxy.at[step, s, t], (SIDES[s], SIDES[t], 0))
            for s in range(2) for t in range(2)
        ]
        return copies

    def interior_x(src, step):
        for c in range(3):
            layers = []
            for x in range(X):
                total = None
                for a in range(-2, 3):
                    if 0 <= x - a < X:
                        term = wgt[0, a + 2, x - a] * src[c, x - a]
                        total = term if total is None else total + term
                layers.append(total)
            for x in range(X):
                cur[c, x] = layers[x]
                for t in range(2):
                    sy[step, t, c, x] = layers[x][(Y - 2) * t:(Y - 2) * t + 2]

    def push_y(step):
        return [push(sy.at[step, t], ry.at[step, t], (0, SIDES[t], 0)) for t in range(2)]

    def put_weights(k):
        for x in range(X):
            for a, w in enumerate(weights(vel[k, x])):
                if k == 1:
                    w = inside(w, a - 2, row, Y)
                if k == 2:
                    w = inside(w, a - 2, lane, Z)
                wgt[k, a, x] = w

    def chunks(values, side):
        held = None
        for c in range(3):
            moved = roll(values[c], 2 * W * (c if side else c + 1), 1)
            held = moved if held is None else jnp.where(lane >= 2 * W * c, moved, held)
        return held

    def unchunk(first, last, c):
        n = first.shape[0]
        low = roll(first, -2 * W * c, 1)
        high = roll(last, Z - 2 * W - 2 * W * c, 1)
        at = lane[:n]
        return jnp.where(at < 2 * W, low, jnp.where(at >= Z - 2 * W, high, 0.0))

    def strip_x(src, step):
        went = []
        for c in range(3):
            u = [qwgt[0, a] * src[c] for a in range(5)]
            keep, go = u[2], None
            for a in (-2, -1, 1, 2):
                moved = roll(u[a + 2], W * a, 1)
                outside = lane < W * a if a > 0 else lane >= W * (X + a)
                keep = keep + jnp.where(outside, 0.0, moved)
                part = jnp.where(outside, moved, 0.0)
                go = part if go is None else go + part
            qcur[c] = keep
            went.append(go)
            for t in range(2):
                syq[step, t, c] = keep[(Y - 2) * t:(Y - 2) * t + 2]
        for s in range(2):
            held = chunks(went, s)
            sxq[step, s, 0] = held
            for t in range(2):
                sxyq[step, s, t] = held[(Y - 2) * t:(Y - 2) * t + 2]

    def push_strip(step):
        n = 2 if step == 0 else 1
        copies = [
            push(sxq.at[step, s, pl.ds(0, n)], rxq.at[step, s, pl.ds(0, n)], (SIDES[s], 0, 0))
            for s in range(2)
        ]
        copies += [
            push(syq.at[step, t, pl.ds(0, 3 * n)], ryq.at[step, t, pl.ds(0, 3 * n)], (0, SIDES[t], 0))
            for t in range(2)
        ]
        copies += [
            push(sxyq.at[step, s, t], rxyq.at[step, s, t], (SIDES[s], SIDES[t], 0))
            for s in range(2) for t in range(2)
        ]
        return copies

    def pass_y(step):
        for c in range(3):
            for x in range(2):
                cur[c, x] += rx[step, 1, c, x]
                cur[c, X - 2 + x] += rx[step, 0, c, x]
        for c in range(3):
            for x in range(X):
                v = cur[c, x]
                total = wgt[1, 2, x] * v
                for a in (-2, -1, 1, 2):
                    total = total + roll(wgt[1, a + 2, x] * v, a, 0)
                low, high = ry[step, 1, c, x], ry[step, 0, c, x]
                if x < 2:
                    low = low + rxy[step, 1, 1, c, x]
                    high = high + rxy[step, 1, 0, c, x]
                if x >= X - 2:
                    low = low + rxy[step, 0, 1, c, x - X + 2]
                    high = high + rxy[step, 0, 0, c, x - X + 2]
                total = pass_z(x, total, low, high)
                cur[c, x] = total

    def ends(total, low, high, w):
        near = w[0] * low
        first = w[1] * low + jnp.concatenate([near[1:2], jnp.zeros_like(near[:1])], 0)
        near = w[2] * high
        last = w[3] * high + jnp.concatenate([jnp.zeros_like(near[:1]), near[0:1]], 0)
        gap = jnp.zeros((Y - 4, Z), jnp.float32)
        return total + jnp.concatenate([first, gap, last], 0)

    def pass_z(x, v, low, high):
        v = ends(v, low, high, [wgt_y[i, x] for i in range(4)])
        total = wgt[2, 2, x] * v
        for a in (-2, -1, 1, 2):
            total = total + roll(wgt[2, a + 2, x] * v, a, 1)
        return total

    def strip_yz(step):
        reach = []
        for c in range(3):
            v = qcur[c] + unchunk(rxq[step, 1, 0], rxq[step, 0, 0], c)
            total = qwgt[1, 2] * v
            for a in (-2, -1, 1, 2):
                total = total + roll(qwgt[1, a + 2] * v, a, 0)
            low = ryq[step, 1, c] + corner(step, 1, c)
            high = ryq[step, 0, c] + corner(step, 0, c)
            v = ends(total, low, high, [qwgt_y[i] for i in range(4)])
            moved = [roll(qwgt[2, a + 2] * v, a, 1) for a in range(-2, 3)]
            low = jnp.where(cell == 4, moved[3], 0.0) + moved[4]
            high = jnp.where(cell == 11, moved[1], 0.0) + moved[0]
            reach.append(jnp.where(cell >= 4, low, roll(high, -8, 1)))
            if step == 0:
                qcur[c] = moved[0] + moved[1] + moved[2] + moved[3] + moved[4]
        return reach

    def corner(step, t, c):
        first = jnp.concatenate([rxyq[step, 1, t]] * 4, 0)
        last = jnp.concatenate([rxyq[step, 0, t]] * 4, 0)
        return unchunk(first, last, c)[:2]

    def slope_rows(v, axis):
        return scale * (
            8.0 * (roll(v, -1, axis) - roll(v, 1, axis)) - (roll(v, -2, axis) - roll(v, 2, axis)))

    def slope_ends(dst, v, low, high):
        top, end = v[0:4], v[Y - 4:Y]
        dst[0:1] = scale * (8.0 * (top[1:2] - low[1:2]) - (top[2:3] - low[0:1]))
        dst[1:2] = scale * (8.0 * (top[2:3] - top[0:1]) - (top[3:4] - low[1:2]))
        dst[Y - 2:Y - 1] = scale * (8.0 * (end[3:4] - end[1:2]) - (high[0:1] - end[0:1]))
        dst[Y - 1:Y] = scale * (8.0 * (high[0:1] - end[2:3]) - (high[1:2] - end[1:2]))

    def slope_x(layers):
        for c in range(3):
            def layer(x):
                if x < 0:
                    return rvx[1, c, x + 2]
                if x >= X:
                    return rvx[0, c, x - X]
                return vel[c, x]
            for x in layers:
                slope[0, c, x] = scale * (
                    8.0 * (layer(x + 1) - layer(x - 1)) - (layer(x + 2) - layer(x - 2)))

    loads[0].wait()
    put_weights(0)
    loads[1].wait()
    spread_x(vort, 0)
    strips = [strip(vort, c) for c in range(3)] + [strip(vel, c) for c in range(3)]
    for m in range(2):
        up = down = None
        for j, s in enumerate(strips[4 * m:4 * m + 4]):
            moved = roll(s, 4 * j, 1), roll(s, 4 * j - 4, 1)
            up = moved[0] if up is None else jnp.where(cell >= 4 * j, moved[0], up)
            down = moved[1] if down is None else jnp.where(cell >= 4 * j, moved[1], down)
        sz[1, m] = up
        sz[0, m] = down
    for c in range(3):
        qvort[c] = jnp.where(cell < 8, strips[c], roll(strips[c], 8, 1))
        qvel[c] = jnp.where(cell < 8, strips[3 + c], roll(strips[3 + c], 8, 1))
    for t in range(2):
        svy[t] = vel[:, :, pl.ds((Y - 2) * t, 2), :]
    pl.semaphore_wait(barrier, len(greeted))
    z_up = push(sz.at[1], rz.at[1], (0, 0, 1))
    from_x = push_x(0)
    vel_y = [push(svy.at[t], rvy.at[t], (0, SIDES[t], 0)) for t in range(2)]
    interior_x(vort, 0)
    from_y = push_y(0)
    vel_x = [
        push(vel.at[:, pl.ds((X - 2) * s, 2)], rvx.at[s], (SIDES[s], 0, 0)) for s in range(2)
    ]
    z_up.wait_recv()
    z_down = push(sz.at[0], rz.at[0], (0, 0, -1))
    put_weights(1)
    put_weights(2)
    for c in range(3):
        for x in range(X):
            slope[1, c, x] = slope_rows(vel[c, x], 0)
            slope[2, c, x] = slope_rows(vel[c, x], 1)
    slope_x(range(2, X - 2))

    z_down.wait_recv()
    for i in range(6):
        m, j = divmod(i, 4)
        low = roll(rz[1, m], -4 * j, 1)
        high = roll(rz[0, m], 12 - 4 * j, 1)
        dst = (qvort if i < 3 else qvel).at[i % 3]
        dst[...] = jnp.where(cell < 4, low, jnp.where(cell >= 12, high, dst[...]))
    for k in range(3):
        for a, w in enumerate(weights(qvel[k])):
            qwgt[k, a] = inside(w, a - 2, row, Y) if k == 1 else w
    strip_x([qvort[c] for c in range(3)], 0)
    for s in range(2):
        sxq[0, s, 1] = chunks([qvel[c] for c in range(3)], 1 - s)
    for t in range(2):
        syq[0, t, pl.ds(3, 3)] = qvel[:, pl.ds((Y - 2) * t, 2), :]
    from_strip = push_strip(0)
    for c in range(3):
        v = qvel[c]
        qslope[1, c] = slope_rows(v, 0)
        qslope[2, c] = slope_rows(v, 1)

    arrived(vel_y)
    for x in range(X):
        low, high = weights(rvy[1, 1, x]), weights(rvy[0, 1, x])
        for i, w in enumerate((low[3], low[4], high[1], high[0])):
            wgt_y[i, x] = w
    for c in range(3):
        for x in range(X):
            slope_ends(slope.at[1, c, x], vel[c, x], rvy[1, c, x], rvy[0, c, x])

    for step in range(SUBSTEPS):
        last = step == SUBSTEPS - 1
        arrived(from_y)
        arrived(from_x)
        pass_y(step)
        if step == 0:
            arrived(vel_x)
            slope_x([0, 1, X - 2, X - 1])
        arrived(from_strip)
        if step == 0:
            low, high = weights(ryq[0, 1, 4]), weights(ryq[0, 0, 4])
            for i, w in enumerate((low[3], low[4], high[1], high[0])):
                qwgt_y[i] = w
        reach = strip_yz(step)
        if step == 0:
            steep = []
            for c in range(3):
                v = qvel[c]
                h = unchunk(rxq[0, 0, 1], rxq[0, 1, 1], c)

                def at(shift):
                    source = roll(v, -W * shift, 1)
                    beyond = lane >= Z - W * shift if shift > 0 else lane < -W * shift
                    return jnp.where(beyond, roll(h, -W * shift, 1), source)

                qslope[0, c] = scale * (8.0 * (at(1) - at(-1)) - (at(2) - at(-2)))
                slope_ends(qslope.at[1, c], v, ryq[0, 1, 3 + c], ryq[0, 0, 3 + c])
                steep.append(jnp.where(cell >= 4, qslope[2, c], roll(qslope[2, c], -8, 1)))
            v = [qcur[c] for c in range(3)]
            for i in range(3):
                total = v[i]
                for j in range(3):
                    total = total + v[j] * qslope[j, i]
                qcur[i] = total

        final = out if last else cur
        order = [0, 1, X - 2, X - 1] + list(range(2, X - 2))
        for n, x in enumerate(order):
            if n == 4 and not last:
                spread_x(cur, step + 1)
                from_x = push_x(step + 1)
            v = [
                cur[c, x] + jnp.where(edge, roll(reach[c], -(W * x + 4), 1), 0.0)
                for c in range(3)
            ]
            if step == 0:
                for c in range(3):
                    slope[2, c, x] = jnp.where(
                        edge, roll(steep[c], -(W * x + 4), 1), slope[2, c, x])
            for i in range(3):
                total = v[i]
                for j in range(3):
                    total = total + v[j] * slope[j, i, x]
                final[i, x] = total
        if not last:
            strip_x([qcur[c] for c in range(3)], step + 1)
            from_strip = push_strip(step + 1)
            interior_x(cur, step + 1)
            from_y = push_y(step + 1)
    for copy in pushed:
        copy.wait_send()


def solution(mesh):
    sizes = [mesh.shape[a] for a in AXES]

    def local(vort, vel):
        _, X, Y, Z = vort.shape
        S = SUBSTEPS

        def V(*shape):
            return pltpu.VMEM(shape, jnp.float32)

        return pl.pallas_call(
            functools.partial(body, sizes),
            out_shape=V(*vort.shape),
            in_specs=[pl.BlockSpec(memory_space=pl.ANY)] * 2,
            out_specs=pl.BlockSpec(memory_space=pltpu.VMEM),
            scratch_shapes=[
                V(3, X, Y, Z), V(3, X, Y, Z),
                V(3, 5, X, Y, Z), V(4, X, 2, Z), V(3, 3, X, Y, Z), V(3, X, Y, Z),
                V(3, Y, Z), V(3, Y, Z), V(3, Y, Z), V(3, 5, Y, Z), V(4, 2, Z), V(3, 3, Y, Z),
                V(S, 2, 3, 2, Y, Z), V(S, 2, 3, 2, Y, Z),
                V(S, 2, 3, X, 2, Z), V(S, 2, 3, X, 2, Z),
                V(S, 2, 2, 3, 2, 2, Z), V(S, 2, 2, 3, 2, 2, Z),
                V(2, 3, 2, Y, Z),
                V(2, 3, X, 2, Z), V(2, 3, X, 2, Z),
                V(2, 2, Y, Z), V(2, 2, Y, Z),
                V(S, 2, 2, Y, Z), V(S, 2, 2, Y, Z),
                V(S, 2, 6, 2, Z), V(S, 2, 6, 2, Z),
                V(S, 2, 2, 2, Z), V(S, 2, 2, 2, Z),
                pltpu.SemaphoreType.DMA((40,)),
                pltpu.SemaphoreType.DMA((40,)),
                pltpu.SemaphoreType.DMA((2,)),
            ],
            compiler_params=pltpu.CompilerParams(collective_id=0, has_side_effects=True),
        )(vort, vel)

    placed = P(None, *AXES)
    return jax.shard_map(
        local, mesh=mesh, in_specs=(placed, placed), out_specs=placed, check_vma=False
    )
```

time: 27.3 us -> 20.9 us (0.77)
  the two profiles are of different devices: /device:TPU:0 before, /device:TPU:25 now
where the time goes in v2:
time: 20.9 us; the launch traced here: 20.7 us
  Pallas kernels  20 us (96%)
  local copies, waits for them, and re-layouts  0.68 us (3%)
    pallas_call x1, Pallas kernels, local(): pl.pallas_call(functools.partial(body, sizes), out_shape=V(*vort.shape),...  20 us
    unnamed x1, local copies, waits for them, and re-layouts  0.68 us

profile of v2, /device:TPU:25, one launch (start us, length us, event | category | flops | bytes accessed | tf_op | source)
XLA Modules:
  0.0 20.7 jit_solution(16444860333885827445)
XLA Ops:
  0.0 20.0 %shard_map.28 = f32[3,8,16,128]{3,2,1,0:T(8,128)S(1)} custom-call(f32[3,8,16,128]{3,2,1,0:T(8,128)} %vort_hbm.1, f32[3,8,16,128]{3,2,1,0:T(8,128)} %vel_hbm.1), custom_call_target="tpu_custom_call" | custom-call | tf_op jit(solution)/shard_map/pallas_call | solution.py:423
  20.0 0.7 %copy.4 = f32[3,8,16,128]{3,2,1,0:T(8,128)} copy(f32[3,8,16,128]{3,2,1,0:T(8,128)S(1)} %shard_map.28) | data formatting | bytes 393216

commit v3 on v2

v3 whole, which is shorter than its diff:
```python
import functools

import jax
import jax.numpy as jnp
from jax import lax
from jax.experimental import pallas as pl
from jax.experimental.pallas import tpu as pltpu
from jax.sharding import PartitionSpec as P

SUBSTEPS = 2
TIME_STEP = 0.5
AXES = ("gx", "gy", "gz")
MESH = pl.DeviceIdType.MESH
SIDES = (-1, 1)


def roll(values, shift, axis):
    shift %= values.shape[axis]
    return pltpu.roll(values, shift, axis) if shift else values


def weights(velocity):
    d = TIME_STEP * velocity
    s = jnp.abs(d)
    t = 1.0 - s
    positive = d > 0.0
    centre = 1.0 + s * s * (1.5 * s - 2.5)
    toward = 1.0 + t * t * (1.5 * t - 2.5)
    away = -0.5 * s * t * t
    beyond = -0.5 * s * s * t
    return (
        jnp.where(positive, 0.0, beyond),
        jnp.where(positive, away, toward),
        centre,
        jnp.where(positive, toward, away),
        jnp.where(positive, beyond, 0.0),
    )


def inside(w, a, index, extent):
    if a == 0:
        return w
    return jnp.where(index < extent - a if a > 0 else index >= -a, w, 0.0)


def body(
    sizes, vort_hbm, vel_hbm, out, vort, vel, wgt, wgt_y, slope, cur,
    strip, ext, wgt_s, slope_s,
    sx, rx, sy, ry, sxy, rxy, rvx, svy, rvy, sz, rz, ssx, rsx, ssy, rsy, ssxy, rsxy,
    send_sem, recv_sem, load_sem,
):
    _, X, Y, Z = vort.shape
    W = 8
    H = 4 * W
    assert (X + 8) * W == Z and 2 * H + X * W == Z and Y >= 8
    scale = TIME_STEP / 12.0
    here = [lax.axis_index(a) for a in AXES]

    def device(*offset):
        return tuple(
            here[k] if not d else lax.rem(here[k] + (d % sizes[k]), sizes[k])
            for k, d in enumerate(offset)
        )

    pushed = []

    def push(src, dst, offset, start=True):
        index = len(pushed)
        copy = pltpu.make_async_remote_copy(
            src_ref=src, dst_ref=dst, send_sem=send_sem.at[index], recv_sem=recv_sem.at[index],
            device_id=device(*offset), device_id_type=MESH,
        )
        if start:
            copy.start()
        pushed.append(copy)
        return copy

    def arrived(copies):
        for copy in copies:
            copy.wait_recv()

    plane = [(dx, dy, 0) for dx in (-1, 0, 1) for dy in (-1, 0, 1) if dx or dy]
    bottom, top = here[2] == 0, here[2] == sizes[2] - 1
    barrier = pltpu.get_barrier_semaphore()

    def greet(offset):
        pl.semaphore_signal(barrier, inc=1, device_id=device(*offset), device_id_type=MESH)

    for offset in plane:
        greet(offset)
    greet((0, 0, -1))

    @pl.when(jnp.logical_not(top))
    def _():
        greet((0, 0, 1))

    loads = [
        pltpu.make_async_copy(vel_hbm, vel, load_sem.at[0]),
        pltpu.make_async_copy(vort_hbm, vort, load_sem.at[1]),
    ]
    for cp in loads:
        cp.start()

    wide = lax.broadcasted_iota(jnp.int32, (Y + 8, Z), 1)
    lane = lax.broadcasted_iota(jnp.int32, (Y, Z), 1)
    row = lax.broadcasted_iota(jnp.int32, (Y, Z), 0)
    cell = lane % W
    edge = (lane < 2) | (lane >= Z - 2)
    rim = (lane < 4) | (lane >= Z - 4)

    def faces(src, c):
        found = roll(src[c, 0], H + 4, 1)
        for x in range(1, X):
            found = jnp.where(lane >= H + W * x, roll(src[c, x], H + W * x + 4, 1), found)
        return found

    def spread_x(src, step, s):
        for c in range(3):
            if s == 0:
                sx[step, 0, c, 0] = wgt[0, 0, 0] * src[c, 0]
                sx[step, 0, c, 1] = wgt[0, 1, 0] * src[c, 0] + wgt[0, 0, 1] * src[c, 1]
            else:
                sx[step, 1, c, 0] = (
                    wgt[0, 3, X - 1] * src[c, X - 1] + wgt[0, 4, X - 2] * src[c, X - 2])
                sx[step, 1, c, 1] = wgt[0, 4, X - 1] * src[c, X - 1]
            for t in range(2):
                sxy[step, s, t, c] = sx[step, s, c, :, pl.ds((Y - 2) * t, 2), :]

    def push_x(step, s):
        return [push(sx.at[step, s], rx.at[step, s], (SIDES[s], 0, 0))] + [
            push(sxy.at[step, s, t], rxy.at[step, s, t], (SIDES[s], SIDES[t], 0))
            for t in range(2)
        ]

    def interior_x(src, step):
        for c in range(3):
            layers = []
            for x in range(X):
                total = None
                for a in range(-2, 3):
                    if 0 <= x - a < X:
                        term = wgt[0, a + 2, x - a] * src[c, x - a]
                        total = term if total is None else total + term
                layers.append(total)
            for x in range(X):
                cur[c, x] = layers[x]
                for t in range(2):
                    sy[step, t, c, x] = layers[x][(Y - 2) * t:(Y - 2) * t + 2]

    def push_y(step):
        return [push(sy.at[step, t], ry.at[step, t], (0, SIDES[t], 0)) for t in range(2)]

    def put_weights(k):
        for x in range(X):
            for a, w in enumerate(weights(vel[k, x])):
                if k == 1:
                    w = inside(w, a - 2, row, Y)
                if k == 2:
                    w = inside(w, a - 2, lane, Z)
                wgt[k, a, x] = w

    def ends(total, low, high, w):
        near = w[0] * low
        first = w[1] * low + jnp.concatenate([near[1:2], jnp.zeros_like(near[:1])], 0)
        near = w[2] * high
        last = w[3] * high + jnp.concatenate([jnp.zeros_like(near[:1]), near[0:1]], 0)
        gap = jnp.zeros((Y - 4, Z), jnp.float32)
        return total + jnp.concatenate([first, gap, last], 0)

    def pass_yz(step, x):
        after = []
        for c in range(3):
            v = cur[c, x]
            low, high = ry[step, 1, c, x], ry[step, 0, c, x]
            for s, i in ((1, x), (0, x - X + 2)):
                if 0 <= i < 2:
                    v = v + rx[step, s, c, i]
                    low = low + rxy[step, s, 1, c, i]
                    high = high + rxy[step, s, 0, c, i]
            total = wgt[1, 2, x] * v
            for a in (-2, -1, 1, 2):
                total = total + roll(wgt[1, a + 2, x] * v, a, 0)
            v = ends(total, low, high, [wgt_y[i, x] for i in range(4)])
            if step > 0:
                v = jnp.where(edge, 0.0, v)
            total = wgt[2, 2, x] * v
            for a in (-2, -1, 1, 2):
                total = total + roll(wgt[2, a + 2, x] * v, a, 1)
            after.append(total)
        return after

    def stretch(v, steepness):
        total = []
        for i in range(3):
            t = v[i]
            for j in range(3):
                t = t + v[j] * steepness(j, i)
            total.append(t)
        return total

    def passes(values, w, axes):
        for k, axis, size in axes:
            total = w(k, 2) * values
            for a in (-2, -1, 1, 2):
                total = total + roll(w(k, a + 2) * values, size * a, axis)
            values = total
        return values

    def slope_rows(v, axis, n=1):
        near = roll(v, -n, axis) - roll(v, n, axis)
        return scale * (8.0 * near - (roll(v, -2 * n, axis) - roll(v, 2 * n, axis)))

    def slope_ends(dst, v, low, high):
        top, end = v[0:4], v[Y - 4:Y]
        dst[0:1] = scale * (8.0 * (top[1:2] - low[1:2]) - (top[2:3] - low[0:1]))
        dst[1:2] = scale * (8.0 * (top[2:3] - top[0:1]) - (top[3:4] - low[1:2]))
        dst[Y - 2:Y - 1] = scale * (8.0 * (end[3:4] - end[1:2]) - (high[0:1] - end[0:1]))
        dst[Y - 1:Y] = scale * (8.0 * (high[0:1] - end[2:3]) - (high[1:2] - end[1:2]))

    def slope_x(layers):
        for c in range(3):
            def layer(x):
                if x < 0:
                    return rvx[1, c, x + 2]
                if x >= X:
                    return rvx[0, c, x - X]
                return vel[c, x]
            for x in layers:
                slope[0, c, x] = scale * (
                    8.0 * (layer(x + 1) - layer(x - 1)) - (layer(x + 2) - layer(x - 2)))

    loads[0].wait()
    put_weights(0)
    loads[1].wait()
    own = [faces(vort, c) for c in range(3)] + [faces(vel, c) for c in range(3)]
    middle = (lane >= H) & (lane < Z - H)
    for i in range(6):
        strip[i] = own[i]
    for m in range(3):
        sz[m] = jnp.where(middle, own[2 * m], roll(own[2 * m + 1], 2 * H, 1))
    for s in (1, 0):
        spread_x(vort, 0, s)
    for t in range(2):
        svy[t] = vel[:, :, pl.ds((Y - 2) * t, 2), :]
    pl.semaphore_wait(barrier, len(plane) + 1 + jnp.where(bottom, 0, 1))
    z_up = push(sz, rz.at[1], (0, 0, 1))
    z_down = push(sz, rz.at[0], (0, 0, -1), start=False)

    @pl.when(jnp.logical_not(bottom))
    def _():
        z_down.start()

    from_x = {}
    for s in (1, 0):
        from_x[s] = push_x(0, s)
        from_x[s].append(
            push(vel.at[:, pl.ds((X - 2) * s, 2)], rvx.at[s], (SIDES[s], 0, 0)))
    vel_y = [push(svy.at[t], rvy.at[t], (0, SIDES[t], 0)) for t in range(2)]
    interior_x(vort, 0)
    from_y = push_y(0)
    put_weights(1)
    put_weights(2)
    for c in range(3):
        for x in range(X):
            slope[1, c, x] = slope_rows(vel[c, x], 0)
            slope[2, c, x] = slope_rows(vel[c, x], 1)
    slope_x(range(2, X - 2))
    arrived(vel_y)
    for x in range(X):
        low, high = weights(rvy[1, 1, x]), weights(rvy[0, 1, x])
        for i, w in enumerate((low[3], low[4], high[1], high[0])):
            wgt_y[i, x] = w
    for c in range(3):
        for x in range(X):
            slope_ends(slope.at[1, c, x], vel[c, x], rvy[1, c, x], rvy[0, c, x])

    z_up.wait_recv()

    @pl.when(bottom)
    def _():
        z_down.start()

    z_down.wait_recv()
    sides = [[], []]
    for i in range(6):
        below, above = [roll(rz[s, i // 2], 2 * H * (i % 2), 1) for s in (1, 0)]
        sides[0].append(jnp.where(cell < 4, below, strip[i]))
        sides[1].append(jnp.where(cell < 4, strip[i], above))
    both = sides[0] + sides[1]
    for i, v in enumerate(both):
        for t in range(2):
            ssy[t, i] = v[(Y - 4) * t:(Y - 4) * t + 4]
        ext[i, pl.ds(4, Y)] = v
    for s in range(2):
        for m in range(3):
            found = None
            for j in range(4):
                moved = roll(both[4 * m + j], H * (j - 1 - s), 1)
                found = moved if found is None else jnp.where(lane >= H * j, moved, found)
            ssx[s, m] = found
            for t in range(2):
                ssxy[s, t, m] = found[(Y - 4) * t:(Y - 4) * t + 4]
    from_strip = [push(ssx.at[s], rsx.at[s], (SIDES[s], 0, 0)) for s in (1, 0)]
    from_strip += [push(ssy.at[t], rsy.at[t], (0, SIDES[t], 0)) for t in range(2)]
    from_strip += [
        push(ssxy.at[s, t], rsxy.at[s, t], (SIDES[s], SIDES[t], 0))
        for s in range(2) for t in range(2)
    ]

    def advance(layers):
        for x in layers:
            v = stretch(pass_yz(0, x), lambda j, i: slope[j, i, x])
            for c in range(3):
                cur[c, x] = v[c]

    arrived(from_y)
    advance(range(2, X - 2))
    onward = {}
    for s, layers in ((1, [0, 1]), (0, [X - 2, X - 1])):
        arrived(from_x[s])
        slope_x(layers)
        advance(layers)
        spread_x(cur, 1, 1 - s)
        onward[1 - s] = push_x(1, 1 - s)
    interior_x(cur, 1)
    from_y = push_y(1)

    arrived(from_strip)
    tip = lane[:8]
    for i in range(12):
        m, j = divmod(i, 4)
        below, above = roll(rsx[1, m], -H * j, 1), roll(rsx[0, m], -H * (j + 1), 1)
        v = ext[i, pl.ds(4, Y)]
        ext[i, pl.ds(4, Y)] = jnp.where(lane < H, below, jnp.where(lane >= Z - H, above, v))
        below, above = [
            roll(jnp.concatenate([rsxy[s, 1, m], rsxy[s, 0, m]], 0), -H * (j + 1 - s), 1)
            for s in (1, 0)
        ]
        v = jnp.concatenate([rsy[1, i], rsy[0, i]], 0)
        v = jnp.where(tip < H, below, jnp.where(tip >= Z - H, above, v))
        ext[i, pl.ds(0, 4)] = v[0:4]
        ext[i, pl.ds(Y + 4, 4)] = v[4:8]
    reach = []
    held = (wide % W >= 2) & (wide % W < 6)
    for side in range(2):
        for k in range(3):
            for a, w in enumerate(weights(ext[6 * side + 3 + k])):
                wgt_s[side, k, a] = w
        for c in range(3):
            v = ext[6 * side + 3 + c]
            for k, (axis, n) in enumerate(((1, W), (0, 1), (1, 1))):
                slope_s[side, k, c] = slope_rows(v, axis, n)

        def w(k, a):
            return wgt_s[side, k, a]

        v = [
            passes(ext[6 * side + c], w, ((0, 1, W), (1, 0, 1), (2, 1, 1))) for c in range(3)
        ]
        v = stretch(v, lambda j, i: slope_s[side, j, i])
        v = [passes(u, w, ((0, 1, W), (1, 0, 1))) for u in v]
        reach.append([passes(jnp.where(held, u, 0.0), w, ((2, 1, 1),))[4:Y + 4] for u in v])
    for c in range(3):
        reach[0][c] = jnp.where(cell >= 4, reach[0][c], reach[1][c])
        steep = jnp.where(
            cell >= 4, slope_s[0, 2, c, pl.ds(4, Y)], slope_s[1, 2, c, pl.ds(4, Y)])
        for x in range(X):
            slope[2, c, x] = jnp.where(edge, roll(steep, -(H + W * x + 4), 1), slope[2, c, x])
    reach = reach[0]

    def settle(layers):
        for x in layers:
            v = pass_yz(1, x)
            for c in range(3):
                cur[c, x] = v[c]

    arrived(from_y)
    settle(range(2, X - 2))
    for s, layers in ((0, [X - 2, X - 1]), (1, [0, 1])):
        arrived(onward[s])
        settle(layers)
    for x in range(X):
        v = [
            cur[c, x] + jnp.where(rim, roll(reach[c], -(H + W * x + 4), 1), 0.0) for c in range(3)
        ]
        v = stretch(v, lambda j, i: slope[j, i, x])
        for c in range(3):
            out[c, x] = v[c]
    for copy in pushed:
        copy.wait_send()


def solution(mesh):
    sizes = [mesh.shape[a] for a in AXES]

    def local(vort, vel):
        _, X, Y, Z = vort.shape
        S = SUBSTEPS

        def V(*shape):
            return pltpu.VMEM(shape, jnp.float32)

        return pl.pallas_call(
            functools.partial(body, sizes),
            out_shape=V(*vort.shape),
            in_specs=[pl.BlockSpec(memory_space=pl.ANY)] * 2,
            out_specs=pl.BlockSpec(memory_space=pltpu.VMEM),
            scratch_shapes=[
                V(3, X, Y, Z), V(3, X, Y, Z),
                V(3, 5, X, Y, Z), V(4, X, 2, Z), V(3, 3, X, Y, Z), V(3, X, Y, Z),
                V(6, Y, Z), V(12, Y + 8, Z), V(2, 3, 5, Y + 8, Z), V(2, 3, 3, Y + 8, Z),
                V(S, 2, 3, 2, Y, Z), V(S, 2, 3, 2, Y, Z),
                V(S, 2, 3, X, 2, Z), V(S, 2, 3, X, 2, Z),
                V(S, 2, 2, 3, 2, 2, Z), V(S, 2, 2, 3, 2, 2, Z),
                V(2, 3, 2, Y, Z),
                V(2, 3, X, 2, Z), V(2, 3, X, 2, Z),
                V(3, Y, Z), V(2, 3, Y, Z),
                V(2, 3, Y, Z), V(2, 3, Y, Z),
                V(2, 12, 4, Z), V(2, 12, 4, Z),
                V(2, 2, 3, 4, Z), V(2, 2, 3, 4, Z),
                pltpu.SemaphoreType.DMA((40,)),
                pltpu.SemaphoreType.DMA((40,)),
                pltpu.SemaphoreType.DMA((2,)),
            ],
            compiler_params=pltpu.CompilerParams(collective_id=0, has_side_effects=True),
        )(vort, vel)

    placed = P(None, *AXES)
    return jax.shard_map(
        local, mesh=mesh, in_specs=(placed, placed), out_specs=placed, check_vma=False
    )
```

time: 20.9 us -> 16.9 us (0.81)
  Pallas kernels: 20 us -> 16.1 us
    pallas_call x1, Pallas kernels: 20 us -> 16.1 us  [local(): pl.pallas_call(functools.partial(body, sizes), out_shape=V(*vort.shape),...]
where the time goes in v3:
time: 16.9 us; the launch traced here: 16.8 us
  Pallas kernels  16.1 us (95%)
  local copies, waits for them, and re-layouts  0.68 us (4%)
    pallas_call x1, Pallas kernels, local(): pl.pallas_call(functools.partial(body, sizes), out_shape=V(*vort.shape),...  16.1 us
    unnamed x1, local copies, waits for them, and re-layouts  0.68 us

profile of v3, /device:TPU:25, one launch (start us, length us, event | category | flops | bytes accessed | tf_op | source)
XLA Modules:
  0.0 16.8 jit_solution(10217122285465985127)
XLA Ops:
  0.0 16.1 %shard_map.28 = f32[3,8,16,128]{3,2,1,0:T(8,128)S(1)} custom-call(f32[3,8,16,128]{3,2,1,0:T(8,128)} %vort_hbm.1, f32[3,8,16,128]{3,2,1,0:T(8,128)} %vel_hbm.1), custom_call_target="tpu_custom_call" | custom-call | tf_op jit(solution)/shard_map/pallas_call | solution.py:403
  16.1 0.7 %copy.4 = f32[3,8,16,128]{3,2,1,0:T(8,128)} copy(f32[3,8,16,128]{3,2,1,0:T(8,128)S(1)} %shard_map.28) | data formatting | bytes 393216

commit v4 on v3

--- a/solution.py
+++ b/solution.py
@@ -12,6 +12,7 @@
 AXES = ("gx", "gy", "gz")
 MESH = pl.DeviceIdType.MESH
 SIDES = (-1, 1)
+COPIES = 46
 
 
 def roll(values, shift, axis):
@@ -45,9 +46,9 @@
 
 def body(
     sizes, vort_hbm, vel_hbm, out, vort, vel, wgt, wgt_y, slope, cur,
-    strip, ext, wgt_s, slope_s,
+    ext, pair, wgt_s, slope_s,
     sx, rx, sy, ry, sxy, rxy, rvx, svy, rvy, sz, rz, ssx, rsx, ssy, rsy, ssxy, rsxy,
-    send_sem, recv_sem, load_sem,
+    send_sem, recv_sem, load_sem, ready,
 ):
     _, X, Y, Z = vort.shape
     W = 8
@@ -114,8 +115,8 @@
             found = jnp.where(lane >= H + W * x, roll(src[c, x], H + W * x + 4, 1), found)
         return found
 
-    def spread_x(src, step, s):
-        for c in range(3):
+    def spread_x(src, step, s, components=range(3)):
+        for c in components:
             if s == 0:
                 sx[step, 0, c, 0] = wgt[0, 0, 0] * src[c, 0]
                 sx[step, 0, c, 1] = wgt[0, 1, 0] * src[c, 0] + wgt[0, 0, 1] * src[c, 1]
@@ -126,11 +127,45 @@
             for t in range(2):
                 sxy[step, s, t, c] = sx[step, s, c, :, pl.ds((Y - 2) * t, 2), :]
 
-    def push_x(step, s):
-        return [push(sx.at[step, s], rx.at[step, s], (SIDES[s], 0, 0))] + [
-            push(sxy.at[step, s, t], rxy.at[step, s, t], (SIDES[s], SIDES[t], 0))
+    def push_x(step, s, part=slice(None)):
+        def piece(ref):
+            return ref if part == slice(None) else ref.at[part]
+
+        return [
+            push(piece(sx.at[step, s]), piece(rx.at[step, s]), (SIDES[s], 0, 0))
+        ] + [
+            push(piece(sxy.at[step, s, t]), piece(rxy.at[step, s, t]), (SIDES[s], SIDES[t], 0))
             for t in range(2)
         ]
+
+    def offer(first, values):
+        for i, v in enumerate(values, first):
+            ext[i, pl.ds(4, Y)] = v
+            for t in range(2):
+                ssy[t, i] = v[(Y - 4) * t:(Y - 4) * t + 4]
+
+    def bundle(m):
+        for s in range(2):
+            found = None
+            for j in range(4):
+                moved = roll(ext[4 * m + j, pl.ds(4, Y)], H * (j - 1 - s), 1)
+                found = moved if found is None else jnp.where(lane >= H * j, moved, found)
+            ssx[s, m] = found
+            for t in range(2):
+                ssxy[s, t, m] = found[(Y - 4) * t:(Y - 4) * t + 4]
+
+    def push_strip(bundles, units):
+        copies = [
+            push(ssx.at[s, bundles], rsx.at[s, bundles], (SIDES[s], 0, 0)) for s in (1, 0)
+        ]
+        copies += [
+            push(ssxy.at[s, t, bundles], rsxy.at[s, t, bundles], (SIDES[s], SIDES[t], 0))
+            for s in (1, 0) for t in range(2)
+        ]
+        copies += [
+            push(ssy.at[t, units], rsy.at[t, units], (0, SIDES[t], 0)) for t in range(2)
+        ]
+        return copies
 
     def interior_x(src, step):
         for c in range(3):
@@ -217,8 +252,8 @@
         dst[Y - 2:Y - 1] = scale * (8.0 * (end[3:4] - end[1:2]) - (high[0:1] - end[0:1]))
         dst[Y - 1:Y] = scale * (8.0 * (high[0:1] - end[2:3]) - (high[1:2] - end[1:2]))
 
-    def slope_x(layers):
-        for c in range(3):
+    def slope_x(layers, components=range(3)):
+        for c in components:
             def layer(x):
                 if x < 0:
                     return rvx[1, c, x + 2]
@@ -234,8 +269,6 @@
     loads[1].wait()
     own = [faces(vort, c) for c in range(3)] + [faces(vel, c) for c in range(3)]
     middle = (lane >= H) & (lane < Z - H)
-    for i in range(6):
-        strip[i] = own[i]
     for m in range(3):
         sz[m] = jnp.where(middle, own[2 * m], roll(own[2 * m + 1], 2 * H, 1))
     for s in (1, 0):
@@ -243,6 +276,11 @@
     for t in range(2):
         svy[t] = vel[:, :, pl.ds((Y - 2) * t, 2), :]
     pl.semaphore_wait(barrier, len(plane) + 1 + jnp.where(bottom, 0, 1))
+
+    @pl.when(top)
+    def _():
+        pl.semaphore_signal(ready, inc=1, device_id=device(0, 0, 1), device_id_type=MESH)
+
     z_up = push(sz, rz.at[1], (0, 0, 1))
     z_down = push(sz, rz.at[0], (0, 0, -1), start=False)
 
@@ -250,14 +288,22 @@
     def _():
         z_down.start()
 
-    from_x = {}
+    from_x, vel_x = {}, {}
     for s in (1, 0):
         from_x[s] = push_x(0, s)
-        from_x[s].append(
-            push(vel.at[:, pl.ds((X - 2) * s, 2)], rvx.at[s], (SIDES[s], 0, 0)))
+        near = pl.ds((X - 2) * s, 2)
+        if s:
+            vel_x[s] = [push(vel.at[:, near], rvx.at[s], (SIDES[s], 0, 0))]
+        else:
+            vel_x[s] = [
+                push(vel.at[c, near], rvx.at[s, c], (SIDES[s], 0, 0)) for c in range(3)
+            ]
     vel_y = [push(svy.at[t], rvy.at[t], (0, SIDES[t], 0)) for t in range(2)]
     interior_x(vort, 0)
     from_y = push_y(0)
+    offer(0, own)
+    bundle(0)
+    from_strip = push_strip(pl.ds(0, 1), pl.ds(0, 6))
     put_weights(1)
     put_weights(2)
     for c in range(3):
@@ -274,38 +320,10 @@
         for x in range(X):
             slope_ends(slope.at[1, c, x], vel[c, x], rvy[1, c, x], rvy[0, c, x])
 
-    z_up.wait_recv()
-
     @pl.when(bottom)
     def _():
+        pl.semaphore_wait(ready, 1)
         z_down.start()
-
-    z_down.wait_recv()
-    sides = [[], []]
-    for i in range(6):
-        below, above = [roll(rz[s, i // 2], 2 * H * (i % 2), 1) for s in (1, 0)]
-        sides[0].append(jnp.where(cell < 4, below, strip[i]))
-        sides[1].append(jnp.where(cell < 4, strip[i], above))
-    both = sides[0] + sides[1]
-    for i, v in enumerate(both):
-        for t in range(2):
-            ssy[t, i] = v[(Y - 4) * t:(Y - 4) * t + 4]
-        ext[i, pl.ds(4, Y)] = v
-    for s in range(2):
-        for m in range(3):
-            found = None
-            for j in range(4):
-                moved = roll(both[4 * m + j], H * (j - 1 - s), 1)
-                found = moved if found is None else jnp.where(lane >= H * j, moved, found)
-            ssx[s, m] = found
-            for t in range(2):
-                ssxy[s, t, m] = found[(Y - 4) * t:(Y - 4) * t + 4]
-    from_strip = [push(ssx.at[s], rsx.at[s], (SIDES[s], 0, 0)) for s in (1, 0)]
-    from_strip += [push(ssy.at[t], rsy.at[t], (0, SIDES[t], 0)) for t in range(2)]
-    from_strip += [
-        push(ssxy.at[s, t], rsxy.at[s, t], (SIDES[s], SIDES[t], 0))
-        for s in range(2) for t in range(2)
-    ]
 
     def advance(layers):
         for x in layers:
@@ -313,15 +331,37 @@
             for c in range(3):
                 cur[c, x] = v[c]
 
+    arrived([z_up, z_down])
+    beyond = []
+    for i in range(6):
+        below, above = [roll(rz[s, i // 2], 2 * H * (i % 2), 1) for s in (1, 0)]
+        beyond.append(jnp.where(cell < 4, below, above))
+    offer(6, beyond)
+    bundle(1)
+    bundle(2)
+    from_strip += push_strip(pl.ds(1, 2), pl.ds(6, 6))
+
     arrived(from_y)
     advance(range(2, X - 2))
-    onward = {}
-    for s, layers in ((1, [0, 1]), (0, [X - 2, X - 1])):
-        arrived(from_x[s])
-        slope_x(layers)
-        advance(layers)
-        spread_x(cur, 1, 1 - s)
-        onward[1 - s] = push_x(1, 1 - s)
+    arrived(from_x[1] + vel_x[1])
+    slope_x([0, 1])
+    advance([0, 1])
+    spread_x(cur, 1, 0)
+    onward = {0: push_x(1, 0), 1: []}
+
+    arrived(from_x[0])
+    rest, along = {}, {}
+    for x in (X - 2, X - 1):
+        v = pass_yz(0, x)
+        along[x] = v[0]
+        rest[x] = [v[i] + v[1] * slope[1, i, x] + v[2] * slope[2, i, x] for i in range(3)]
+    for c in range(3):
+        arrived([vel_x[0][c]])
+        slope_x([X - 2, X - 1], [c])
+        for x in (X - 2, X - 1):
+            cur[c, x] = rest[x][c] + along[x] * slope[0, c, x]
+        spread_x(cur, 1, 1, [c])
+        onward[1] += push_x(1, 1, c)
     interior_x(cur, 1)
     from_y = push_y(1)
 
@@ -340,52 +380,50 @@
         v = jnp.where(tip < H, below, jnp.where(tip >= Z - H, above, v))
         ext[i, pl.ds(0, 4)] = v[0:4]
         ext[i, pl.ds(Y + 4, 4)] = v[4:8]
-    reach = []
-    held = (wide % W >= 2) & (wide % W < 6)
-    for side in range(2):
-        for k in range(3):
-            for a, w in enumerate(weights(ext[6 * side + 3 + k])):
-                wgt_s[side, k, a] = w
-        for c in range(3):
-            v = ext[6 * side + 3 + c]
-            for k, (axis, n) in enumerate(((1, W), (0, 1), (1, 1))):
-                slope_s[side, k, c] = slope_rows(v, axis, n)
-
-        def w(k, a):
-            return wgt_s[side, k, a]
-
-        v = [
-            passes(ext[6 * side + c], w, ((0, 1, W), (1, 0, 1), (2, 1, 1))) for c in range(3)
-        ]
-        v = stretch(v, lambda j, i: slope_s[side, j, i])
-        v = [passes(u, w, ((0, 1, W), (1, 0, 1))) for u in v]
-        reach.append([passes(jnp.where(held, u, 0.0), w, ((2, 1, 1),))[4:Y + 4] for u in v])
+    inner = wide % W
+    held = (inner >= 2) & (inner < 6)
+    for i in range(6):
+        pair[i, 0] = jnp.where(inner < 4, ext[6 + i], ext[i])
+        pair[i, 1] = jnp.where(inner < 4, ext[i], ext[6 + i])
+    for k in range(3):
+        for a, w in enumerate(weights(pair[3 + k])):
+            wgt_s[k, a] = w
     for c in range(3):
-        reach[0][c] = jnp.where(cell >= 4, reach[0][c], reach[1][c])
+        v = pair[3 + c]
+        for k, (axis, n) in enumerate(((2, W), (1, 1), (2, 1))):
+            slope_s[k, c] = slope_rows(v, axis, n)
+
+    def w(k, a):
+        return wgt_s[k, a]
+
+    in_x, in_y, in_z = (0, 2, W), (1, 1, 1), (2, 2, 1)
+    v = [passes(pair[c], w, (in_x, in_y, in_z)) for c in range(3)]
+    v = stretch(v, lambda j, i: slope_s[j, i])
+    v = [passes(u, w, (in_x, in_y)) for u in v]
+    v = [passes(jnp.where(held, u, 0.0), w, (in_z,)) for u in v]
+    reach = [jnp.where(cell >= 4, u[0, 4:Y + 4], u[1, 4:Y + 4]) for u in v]
+    for c in range(3):
         steep = jnp.where(
-            cell >= 4, slope_s[0, 2, c, pl.ds(4, Y)], slope_s[1, 2, c, pl.ds(4, Y)])
+            cell >= 4, slope_s[2, c, 0, pl.ds(4, Y)], slope_s[2, c, 1, pl.ds(4, Y)])
         for x in range(X):
             slope[2, c, x] = jnp.where(edge, roll(steep, -(H + W * x + 4), 1), slope[2, c, x])
-    reach = reach[0]
 
     def settle(layers):
         for x in layers:
-            v = pass_yz(1, x)
+            v = [
+                u + jnp.where(rim, roll(reach[c], -(H + W * x + 4), 1), 0.0)
+                for c, u in enumerate(pass_yz(1, x))
+            ]
+            v = stretch(v, lambda j, i: slope[j, i, x])
             for c in range(3):
-                cur[c, x] = v[c]
+                out[c, x] = v[c]
 
     arrived(from_y)
     settle(range(2, X - 2))
     for s, layers in ((0, [X - 2, X - 1]), (1, [0, 1])):
         arrived(onward[s])
         settle(layers)
-    for x in range(X):
-        v = [
-            cur[c, x] + jnp.where(rim, roll(reach[c], -(H + W * x + 4), 1), 0.0) for c in range(3)
-        ]
-        v = stretch(v, lambda j, i: slope[j, i, x])
-        for c in range(3):
-            out[c, x] = v[c]
+    assert len(pushed) == COPIES
     for copy in pushed:
         copy.wait_send()
 
@@ -408,7 +446,7 @@
             scratch_shapes=[
                 V(3, X, Y, Z), V(3, X, Y, Z),
                 V(3, 5, X, Y, Z), V(4, X, 2, Z), V(3, 3, X, Y, Z), V(3, X, Y, Z),
-                V(6, Y, Z), V(12, Y + 8, Z), V(2, 3, 5, Y + 8, Z), V(2, 3, 3, Y + 8, Z),
+                V(12, Y + 8, Z), V(6, 2, Y + 8, Z), V(3, 5, 2, Y + 8, Z), V(3, 3, 2, Y + 8, Z),
                 V(S, 2, 3, 2, Y, Z), V(S, 2, 3, 2, Y, Z),
                 V(S, 2, 3, X, 2, Z), V(S, 2, 3, X, 2, Z),
                 V(S, 2, 2, 3, 2, 2, Z), V(S, 2, 2, 3, 2, 2, Z),
@@ -418,9 +456,10 @@
                 V(2, 3, Y, Z), V(2, 3, Y, Z),
                 V(2, 12, 4, Z), V(2, 12, 4, Z),
                 V(2, 2, 3, 4, Z), V(2, 2, 3, 4, Z),
-                pltpu.SemaphoreType.DMA((40,)),
-                pltpu.SemaphoreType.DMA((40,)),
+                pltpu.SemaphoreType.DMA((COPIES,)),
+                pltpu.SemaphoreType.DMA((COPIES,)),
                 pltpu.SemaphoreType.DMA((2,)),
+                pltpu.SemaphoreType.REGULAR,
             ],
             compiler_params=pltpu.CompilerParams(collective_id=0, has_side_effects=True),
         )(vort, vel)

time: 16.9 us -> 16.3 us (0.964)
  the two profiles are of different devices: /device:TPU:25 before, /device:TPU:0 now
where the time goes in v4:
time: 16.3 us; the launch traced here: 16.1 us
  Pallas kernels  15.5 us (95%)
  local copies, waits for them, and re-layouts  0.68 us (4%)
    pallas_call x1, Pallas kernels, local(): pl.pallas_call(functools.partial(body, sizes), out_shape=V(*vort.shape),...  15.5 us
    unnamed x1, local copies, waits for them, and re-layouts  0.68 us

profile of v4, /device:TPU:0, one launch (start us, length us, event | category | flops | bytes accessed | tf_op | source)
XLA Modules:
  0.0 16.1 jit_solution(8562186650912209386)
XLA Ops:
  0.0 15.5 %shard_map.28 = f32[3,8,16,128]{3,2,1,0:T(8,128)S(1)} custom-call(f32[3,8,16,128]{3,2,1,0:T(8,128)} %vort_hbm.1, f32[3,8,16,128]{3,2,1,0:T(8,128)} %vel_hbm.1), custom_call_target="tpu_custom_call" | custom-call | tf_op jit(solution)/shard_map/pallas_call | solution.py:441
  15.5 0.7 %copy.4 = f32[3,8,16,128]{3,2,1,0:T(8,128)} copy(f32[3,8,16,128]{3,2,1,0:T(8,128)S(1)} %shard_map.28) | data formatting | bytes 393216

commit v5 on v4

--- a/solution.py
+++ b/solution.py
@@ -1,4 +1,5 @@
 import functools
+import math
 
 import jax
 import jax.numpy as jnp
@@ -12,7 +13,7 @@
 AXES = ("gx", "gy", "gz")
 MESH = pl.DeviceIdType.MESH
 SIDES = (-1, 1)
-COPIES = 46
+GROUPS = 12
 
 
 def roll(values, shift, axis):
@@ -48,7 +49,7 @@
     sizes, vort_hbm, vel_hbm, out, vort, vel, wgt, wgt_y, slope, cur,
     ext, pair, wgt_s, slope_s,
     sx, rx, sy, ry, sxy, rxy, rvx, svy, rvy, sz, rz, ssx, rsx, ssy, rsy, ssxy, rsxy,
-    send_sem, recv_sem, load_sem, ready,
+    total, send_sem, recv_sem, load_sem, ready,
 ):
     _, X, Y, Z = vort.shape
     W = 8
@@ -63,22 +64,29 @@
             for k, d in enumerate(offset)
         )
 
-    pushed = []
-
-    def push(src, dst, offset, start=True):
-        index = len(pushed)
+    rows = {}
+
+    def push(src, dst, offset, group, start=True):
+        rows.setdefault(group, 0)
+        rows[group] += math.prod(src.shape[:-1])
         copy = pltpu.make_async_remote_copy(
-            src_ref=src, dst_ref=dst, send_sem=send_sem.at[index], recv_sem=recv_sem.at[index],
+            src_ref=src, dst_ref=dst, send_sem=send_sem.at[0],
+            recv_sem=recv_sem.at[list(rows).index(group)],
             device_id=device(*offset), device_id_type=MESH,
         )
         if start:
             copy.start()
-        pushed.append(copy)
         return copy
 
-    def arrived(copies):
-        for copy in copies:
-            copy.wait_recv()
+    def tally(n, group=0):
+        some = total.at[pl.ds(0, n)]
+        return pltpu.make_async_remote_copy(
+            src_ref=some, dst_ref=some, send_sem=send_sem.at[0], recv_sem=recv_sem.at[group],
+            device_id=device(1, 0, 0), device_id_type=MESH,
+        )
+
+    def arrived(group):
+        tally(rows[group], list(rows).index(group)).wait_recv()
 
     plane = [(dx, dy, 0) for dx in (-1, 0, 1) for dy in (-1, 0, 1) if dx or dy]
     bottom, top = here[2] == 0, here[2] == sizes[2] - 1
@@ -127,16 +135,15 @@
             for t in range(2):
                 sxy[step, s, t, c] = sx[step, s, c, :, pl.ds((Y - 2) * t, 2), :]
 
-    def push_x(step, s, part=slice(None)):
+    def push_x(step, s, group, part=slice(None)):
         def piece(ref):
             return ref if part == slice(None) else ref.at[part]
 
-        return [
-            push(piece(sx.at[step, s]), piece(rx.at[step, s]), (SIDES[s], 0, 0))
-        ] + [
-            push(piece(sxy.at[step, s, t]), piece(rxy.at[step, s, t]), (SIDES[s], SIDES[t], 0))
-            for t in range(2)
-        ]
+        push(piece(sx.at[step, s]), piece(rx.at[step, s]), (SIDES[s], 0, 0), group)
+        for t in range(2):
+            push(
+                piece(sxy.at[step, s, t]), piece(rxy.at[step, s, t]), (SIDES[s], SIDES[t], 0),
+                group)
 
     def offer(first, values):
         for i, v in enumerate(values, first):
@@ -155,17 +162,14 @@
                 ssxy[s, t, m] = found[(Y - 4) * t:(Y - 4) * t + 4]
 
     def push_strip(bundles, units):
-        copies = [
-            push(ssx.at[s, bundles], rsx.at[s, bundles], (SIDES[s], 0, 0)) for s in (1, 0)
-        ]
-        copies += [
-            push(ssxy.at[s, t, bundles], rsxy.at[s, t, bundles], (SIDES[s], SIDES[t], 0))
-            for s in (1, 0) for t in range(2)
-        ]
-        copies += [
-            push(ssy.at[t, units], rsy.at[t, units], (0, SIDES[t], 0)) for t in range(2)
-        ]
-        return copies
+        for s in (1, 0):
+            push(ssx.at[s, bundles], rsx.at[s, bundles], (SIDES[s], 0, 0), "strip")
+            for t in range(2):
+                push(
+                    ssxy.at[s, t, bundles], rsxy.at[s, t, bundles], (SIDES[s], SIDES[t], 0),
+                    "strip")
+        for t in range(2):
+            push(ssy.at[t, units], rsy.at[t, units], (0, SIDES[t], 0), "strip")
 
     def interior_x(src, step):
         for c in range(3):
@@ -183,10 +187,11 @@
                     sy[step, t, c, x] = layers[x][(Y - 2) * t:(Y - 2) * t + 2]
 
     def push_y(step):
-        return [push(sy.at[step, t], ry.at[step, t], (0, SIDES[t], 0)) for t in range(2)]
-
-    def put_weights(k):
-        for x in range(X):
+        for t in range(2):
+            push(sy.at[step, t], ry.at[step, t], (0, SIDES[t], 0), f"y{step}")
+
+    def put_weights(k, layers):
+        for x in layers:
             for a, w in enumerate(weights(vel[k, x])):
                 if k == 1:
                     w = inside(w, a - 2, row, Y)
@@ -265,53 +270,52 @@
                     8.0 * (layer(x + 1) - layer(x - 1)) - (layer(x + 2) - layer(x - 2)))
 
     loads[0].wait()
-    put_weights(0)
+    put_weights(0, [0, 1, X - 2, X - 1])
     loads[1].wait()
+    for s in (1, 0):
+        spread_x(vort, 0, s)
+    pl.semaphore_wait(barrier, len(plane) + 1 + jnp.where(bottom, 0, 1))
+
+    @pl.when(top)
+    def _():
+        pl.semaphore_signal(ready, inc=1, device_id=device(0, 0, 1), device_id_type=MESH)
+
+    for s in (1, 0):
+        push_x(0, s, f"x{s}")
+        near = pl.ds((X - 2) * s, 2)
+        if s:
+            push(vel.at[:, near], rvx.at[s], (SIDES[s], 0, 0), "x1")
+        else:
+            for c in range(3):
+                push(vel.at[c, near], rvx.at[s, c], (SIDES[s], 0, 0), f"vel{c}")
     own = [faces(vort, c) for c in range(3)] + [faces(vel, c) for c in range(3)]
     middle = (lane >= H) & (lane < Z - H)
     for m in range(3):
         sz[m] = jnp.where(middle, own[2 * m], roll(own[2 * m + 1], 2 * H, 1))
-    for s in (1, 0):
-        spread_x(vort, 0, s)
-    for t in range(2):
-        svy[t] = vel[:, :, pl.ds((Y - 2) * t, 2), :]
-    pl.semaphore_wait(barrier, len(plane) + 1 + jnp.where(bottom, 0, 1))
-
-    @pl.when(top)
-    def _():
-        pl.semaphore_signal(ready, inc=1, device_id=device(0, 0, 1), device_id_type=MESH)
-
-    z_up = push(sz, rz.at[1], (0, 0, 1))
-    z_down = push(sz, rz.at[0], (0, 0, -1), start=False)
+    push(sz, rz.at[1], (0, 0, 1), "z")
+    z_down = push(sz, rz.at[0], (0, 0, -1), "z", start=False)
 
     @pl.when(jnp.logical_not(bottom))
     def _():
         z_down.start()
 
-    from_x, vel_x = {}, {}
-    for s in (1, 0):
-        from_x[s] = push_x(0, s)
-        near = pl.ds((X - 2) * s, 2)
-        if s:
-            vel_x[s] = [push(vel.at[:, near], rvx.at[s], (SIDES[s], 0, 0))]
-        else:
-            vel_x[s] = [
-                push(vel.at[c, near], rvx.at[s, c], (SIDES[s], 0, 0)) for c in range(3)
-            ]
-    vel_y = [push(svy.at[t], rvy.at[t], (0, SIDES[t], 0)) for t in range(2)]
+    for t in range(2):
+        svy[t] = vel[:, :, pl.ds((Y - 2) * t, 2), :]
+        push(svy.at[t], rvy.at[t], (0, SIDES[t], 0), "vel_y")
+    put_weights(0, range(2, X - 2))
     interior_x(vort, 0)
-    from_y = push_y(0)
+    push_y(0)
     offer(0, own)
     bundle(0)
-    from_strip = push_strip(pl.ds(0, 1), pl.ds(0, 6))
-    put_weights(1)
-    put_weights(2)
+    push_strip(pl.ds(0, 1), pl.ds(0, 6))
+    put_weights(1, range(X))
+    put_weights(2, range(X))
     for c in range(3):
         for x in range(X):
             slope[1, c, x] = slope_rows(vel[c, x], 0)
             slope[2, c, x] = slope_rows(vel[c, x], 1)
     slope_x(range(2, X - 2))
-    arrived(vel_y)
+    arrived("vel_y")
     for x in range(X):
         low, high = weights(rvy[1, 1, x]), weights(rvy[0, 1, x])
         for i, w in enumerate((low[3], low[4], high[1], high[0])):
@@ -331,7 +335,7 @@
             for c in range(3):
                 cur[c, x] = v[c]
 
-    arrived([z_up, z_down])
+    arrived("z")
     beyond = []
     for i in range(6):
         below, above = [roll(rz[s, i // 2], 2 * H * (i % 2), 1) for s in (1, 0)]
@@ -339,33 +343,33 @@
     offer(6, beyond)
     bundle(1)
     bundle(2)
-    from_strip += push_strip(pl.ds(1, 2), pl.ds(6, 6))
-
-    arrived(from_y)
+    push_strip(pl.ds(1, 2), pl.ds(6, 6))
+
+    arrived("y0")
     advance(range(2, X - 2))
-    arrived(from_x[1] + vel_x[1])
+    arrived("x1")
     slope_x([0, 1])
     advance([0, 1])
     spread_x(cur, 1, 0)
-    onward = {0: push_x(1, 0), 1: []}
-
-    arrived(from_x[0])
+    push_x(1, 0, "x0 again")
+
+    arrived("x0")
     rest, along = {}, {}
     for x in (X - 2, X - 1):
         v = pass_yz(0, x)
         along[x] = v[0]
         rest[x] = [v[i] + v[1] * slope[1, i, x] + v[2] * slope[2, i, x] for i in range(3)]
     for c in range(3):
-        arrived([vel_x[0][c]])
+        arrived(f"vel{c}")
         slope_x([X - 2, X - 1], [c])
         for x in (X - 2, X - 1):
             cur[c, x] = rest[x][c] + along[x] * slope[0, c, x]
         spread_x(cur, 1, 1, [c])
-        onward[1] += push_x(1, 1, c)
+        push_x(1, 1, "x1 again", c)
     interior_x(cur, 1)
-    from_y = push_y(1)
-
-    arrived(from_strip)
+    push_y(1)
+
+    arrived("strip")
     tip = lane[:8]
     for i in range(12):
         m, j = divmod(i, 4)
@@ -418,14 +422,13 @@
             for c in range(3):
                 out[c, x] = v[c]
 
-    arrived(from_y)
+    arrived("y1")
     settle(range(2, X - 2))
     for s, layers in ((0, [X - 2, X - 1]), (1, [0, 1])):
-        arrived(onward[s])
+        arrived(f"x{s} again")
         settle(layers)
-    assert len(pushed) == COPIES
-    for copy in pushed:
-        copy.wait_send()
+    assert len(rows) == GROUPS and sum(rows.values()) == total.shape[0]
+    tally(sum(rows.values())).wait_send()
 
 
 def solution(mesh):
@@ -456,8 +459,9 @@
                 V(2, 3, Y, Z), V(2, 3, Y, Z),
                 V(2, 12, 4, Z), V(2, 12, 4, Z),
                 V(2, 2, 3, 4, Z), V(2, 2, 3, 4, Z),
-                pltpu.SemaphoreType.DMA((COPIES,)),
-                pltpu.SemaphoreType.DMA((COPIES,)),
+                V(48 * Y + 36 * X + 240, 1, Z),
+                pltpu.SemaphoreType.DMA((1,)),
+                pltpu.SemaphoreType.DMA((GROUPS,)),
                 pltpu.SemaphoreType.DMA((2,)),
                 pltpu.SemaphoreType.REGULAR,
             ],

time: 16.3 us -> 15.5 us (0.951)
  Pallas kernels: 15.5 us -> 14.7 us
    pallas_call x1, Pallas kernels: 15.5 us -> 14.7 us  [local(): pl.pallas_call(functools.partial(body, sizes), out_shape=V(*vort.shape),...]
where the time goes in v5:
time: 15.5 us; the launch traced here: 15.4 us
  Pallas kernels  14.7 us (95%)
  local copies, waits for them, and re-layouts  0.68 us (4%)
    pallas_call x1, Pallas kernels, local(): pl.pallas_call(functools.partial(body, sizes), out_shape=V(*vort.shape),...  14.7 us
    unnamed x1, local copies, waits for them, and re-layouts  0.68 us

profile of v5, /device:TPU:0, one launch (start us, length us, event | category | flops | bytes accessed | tf_op | source)
XLA Modules:
  0.0 15.4 jit_solution(16257991902475033338)
XLA Ops:
  0.0 14.7 %shard_map.28 = f32[3,8,16,128]{3,2,1,0:T(8,128)S(1)} custom-call(f32[3,8,16,128]{3,2,1,0:T(8,128)} %vort_hbm.1, f32[3,8,16,128]{3,2,1,0:T(8,128)} %vel_hbm.1), custom_call_target="tpu_custom_call" | custom-call | tf_op jit(solution)/shard_map/pallas_call | solution.py:444
  14.7 0.7 %copy.4 = f32[3,8,16,128]{3,2,1,0:T(8,128)} copy(f32[3,8,16,128]{3,2,1,0:T(8,128)S(1)} %shard_map.28) | data formatting | bytes 393216

commit v6 on v5

--- a/solution.py
+++ b/solution.py
@@ -13,7 +13,7 @@
 AXES = ("gx", "gy", "gz")
 MESH = pl.DeviceIdType.MESH
 SIDES = (-1, 1)
-GROUPS = 12
+GROUPS = 14
 
 
 def roll(values, shift, axis):
@@ -88,27 +88,27 @@
     def arrived(group):
         tally(rows[group], list(rows).index(group)).wait_recv()
 
-    plane = [(dx, dy, 0) for dx in (-1, 0, 1) for dy in (-1, 0, 1) if dx or dy]
-    bottom, top = here[2] == 0, here[2] == sizes[2] - 1
-    barrier = pltpu.get_barrier_semaphore()
-
-    def greet(offset):
-        pl.semaphore_signal(barrier, inc=1, device_id=device(*offset), device_id_type=MESH)
-
-    for offset in plane:
-        greet(offset)
-    greet((0, 0, -1))
-
-    @pl.when(jnp.logical_not(top))
-    def _():
-        greet((0, 0, 1))
-
     loads = [
         pltpu.make_async_copy(vel_hbm, vel, load_sem.at[0]),
         pltpu.make_async_copy(vort_hbm, vort, load_sem.at[1]),
     ]
     for cp in loads:
         cp.start()
+
+    plane = [(dx, dy, 0) for dx in (-1, 0, 1) for dy in (-1, 0, 1) if dx or dy]
+    bottom, top = here[2] == 0, here[2] == sizes[2] - 1
+    barrier = pltpu.get_barrier_semaphore()
+
+    def greet(offset):
+        pl.semaphore_signal(barrier, inc=1, device_id=device(*offset), device_id_type=MESH)
+
+    for offset in plane:
+        greet(offset)
+    greet((0, 0, -1))
+
+    @pl.when(jnp.logical_not(top))
+    def _():
+        greet((0, 0, 1))
 
     wide = lax.broadcasted_iota(jnp.int32, (Y + 8, Z), 1)
     lane = lax.broadcasted_iota(jnp.int32, (Y, Z), 1)
@@ -207,9 +207,9 @@
         gap = jnp.zeros((Y - 4, Z), jnp.float32)
         return total + jnp.concatenate([first, gap, last], 0)
 
-    def pass_yz(step, x):
+    def pass_yz(step, x, components=range(3)):
         after = []
-        for c in range(3):
+        for c in components:
             v = cur[c, x]
             low, high = ry[step, 1, c, x], ry[step, 0, c, x]
             for s, i in ((1, x), (0, x - X + 2)):
@@ -274,11 +274,31 @@
     loads[1].wait()
     for s in (1, 0):
         spread_x(vort, 0, s)
+    own = [faces(vort, c) for c in range(3)] + [faces(vel, c) for c in range(3)]
+    middle = (lane >= H) & (lane < Z - H)
+    for m in range(2):
+        for up in range(2):
+            found = None
+            for j, v in enumerate(own[4 * m:4 * m + 4]):
+                h, late = j % 2, j // 2
+                moved = roll(v, 2 * H * h + 4 * (late - 1 + up), 1)
+                spot = middle == (h == 0)
+                if late:
+                    spot = spot & (cell >= 4)
+                found = moved if found is None else jnp.where(spot, moved, found)
+            sz[up, m] = found
     pl.semaphore_wait(barrier, len(plane) + 1 + jnp.where(bottom, 0, 1))
 
     @pl.when(top)
     def _():
         pl.semaphore_signal(ready, inc=1, device_id=device(0, 0, 1), device_id_type=MESH)
+
+    push(sz.at[1], rz.at[1], (0, 0, 1), "z")
+    z_down = push(sz.at[0], rz.at[0], (0, 0, -1), "z", start=False)
+
+    @pl.when(jnp.logical_not(bottom))
+    def _():
+        z_down.start()
 
     for s in (1, 0):
         push_x(0, s, f"x{s}")
@@ -288,17 +308,6 @@
         else:
             for c in range(3):
                 push(vel.at[c, near], rvx.at[s, c], (SIDES[s], 0, 0), f"vel{c}")
-    own = [faces(vort, c) for c in range(3)] + [faces(vel, c) for c in range(3)]
-    middle = (lane >= H) & (lane < Z - H)
-    for m in range(3):
-        sz[m] = jnp.where(middle, own[2 * m], roll(own[2 * m + 1], 2 * H, 1))
-    push(sz, rz.at[1], (0, 0, 1), "z")
-    z_down = push(sz, rz.at[0], (0, 0, -1), "z", start=False)
-
-    @pl.when(jnp.logical_not(bottom))
-    def _():
-        z_down.start()
-
     for t in range(2):
         svy[t] = vel[:, :, pl.ds((Y - 2) * t, 2), :]
         push(svy.at[t], rvy.at[t], (0, SIDES[t], 0), "vel_y")
@@ -338,7 +347,9 @@
     arrived("z")
     beyond = []
     for i in range(6):
-        below, above = [roll(rz[s, i // 2], 2 * H * (i % 2), 1) for s in (1, 0)]
+        h, late = i % 2, i % 4 // 2
+        below = roll(rz[1, i // 4], 2 * H * h - 4 * late, 1)
+        above = roll(rz[0, i // 4], 2 * H * h + 4 - 4 * late, 1)
         beyond.append(jnp.where(cell < 4, below, above))
     offer(6, beyond)
     bundle(1)
@@ -365,7 +376,7 @@
         for x in (X - 2, X - 1):
             cur[c, x] = rest[x][c] + along[x] * slope[0, c, x]
         spread_x(cur, 1, 1, [c])
-        push_x(1, 1, "x1 again", c)
+        push_x(1, 1, f"x1 again{c}", c)
     interior_x(cur, 1)
     push_y(1)
 
@@ -424,9 +435,19 @@
 
     arrived("y1")
     settle(range(2, X - 2))
-    for s, layers in ((0, [X - 2, X - 1]), (1, [0, 1])):
-        arrived(f"x{s} again")
-        settle(layers)
+    arrived("x0 again")
+    settle([X - 2, X - 1])
+    late = {0: [], 1: []}
+    for c in range(3):
+        arrived(f"x1 again{c}")
+        for x in (0, 1):
+            late[x].append(
+                pass_yz(1, x, [c])[0]
+                + jnp.where(rim, roll(reach[c], -(H + W * x + 4), 1), 0.0))
+    for x in (0, 1):
+        v = stretch(late[x], lambda j, i: slope[j, i, x])
+        for c in range(3):
+            out[c, x] = v[c]
     assert len(rows) == GROUPS and sum(rows.values()) == total.shape[0]
     tally(sum(rows.values())).wait_send()
 
@@ -455,11 +476,11 @@
                 V(S, 2, 2, 3, 2, 2, Z), V(S, 2, 2, 3, 2, 2, Z),
                 V(2, 3, 2, Y, Z),
                 V(2, 3, X, 2, Z), V(2, 3, X, 2, Z),
-                V(3, Y, Z), V(2, 3, Y, Z),
+                V(2, 2, Y, Z), V(2, 2, Y, Z),
                 V(2, 3, Y, Z), V(2, 3, Y, Z),
                 V(2, 12, 4, Z), V(2, 12, 4, Z),
                 V(2, 2, 3, 4, Z), V(2, 2, 3, 4, Z),
-                V(48 * Y + 36 * X + 240, 1, Z),
+                V(46 * Y + 36 * X + 240, 1, Z),
                 pltpu.SemaphoreType.DMA((1,)),
                 pltpu.SemaphoreType.DMA((GROUPS,)),
                 pltpu.SemaphoreType.DMA((2,)),

time: 15.5 us -> 15.5 us (level)
  no operation moved by 1% of the time
where the time goes in v6:
time: 15.5 us; the launch traced here: 15.3 us
  Pallas kernels  14.6 us (94%)
  local copies, waits for them, and re-layouts  0.68 us (4%)
    pallas_call x1, Pallas kernels, local(): pl.pallas_call(functools.partial(body, sizes), out_shape=V(*vort.shape),...  14.6 us
    unnamed x1, local copies, waits for them, and re-layouts  0.68 us

profile of v6, /device:TPU:0, one launch (start us, length us, event | category | flops | bytes accessed | tf_op | source)
XLA Modules:
  0.0 15.3 jit_solution(6496897634356076307)
XLA Ops:
  0.0 14.6 %shard_map.28 = f32[3,8,16,128]{3,2,1,0:T(8,128)S(1)} custom-call(f32[3,8,16,128]{3,2,1,0:T(8,128)} %vort_hbm.1, f32[3,8,16,128]{3,2,1,0:T(8,128)} %vel_hbm.1), custom_call_target="tpu_custom_call" | custom-call | tf_op jit(solution)/shard_map/pallas_call | solution.py:465
  14.6 0.7 %copy.4 = f32[3,8,16,128]{3,2,1,0:T(8,128)} copy(f32[3,8,16,128]{3,2,1,0:T(8,128)S(1)} %shard_map.28) | data formatting | bytes 393216

commit v7 on v6

--- a/solution.py
+++ b/solution.py
@@ -379,6 +379,14 @@
         push_x(1, 1, f"x1 again{c}", c)
     interior_x(cur, 1)
     push_y(1)
+
+    for c in range(3):
+        mine, other = ext[3 + c, pl.ds(4, Y)], ext[9 + c, pl.ds(4, Y)]
+        left = slope_rows(jnp.where(cell < 4, other, mine), 1)
+        right = slope_rows(jnp.where(cell < 4, mine, other), 1)
+        steep = jnp.where(cell >= 4, left, right)
+        for x in range(X):
+            slope[2, c, x] = jnp.where(edge, roll(steep, -(H + W * x + 4), 1), slope[2, c, x])
 
     arrived("strip")
     tip = lane[:8]
@@ -417,12 +425,6 @@
     v = [passes(u, w, (in_x, in_y)) for u in v]
     v = [passes(jnp.where(held, u, 0.0), w, (in_z,)) for u in v]
     reach = [jnp.where(cell >= 4, u[0, 4:Y + 4], u[1, 4:Y + 4]) for u in v]
-    for c in range(3):
-        steep = jnp.where(
-            cell >= 4, slope_s[2, c, 0, pl.ds(4, Y)], slope_s[2, c, 1, pl.ds(4, Y)])
-        for x in range(X):
-            slope[2, c, x] = jnp.where(edge, roll(steep, -(H + W * x + 4), 1), slope[2, c, x])
-
     def settle(layers):
         for x in layers:
             v = [

time: 15.5 us -> 15.5 us (level)
  no operation moved by 1% of the time
where the time goes in v7:
time: 15.5 us; the launch traced here: 15.3 us
  Pallas kernels  14.6 us (94%)
  local copies, waits for them, and re-layouts  0.68 us (4%)
    pallas_call x1, Pallas kernels, local(): pl.pallas_call(functools.partial(body, sizes), out_shape=V(*vort.shape),...  14.6 us
    unnamed x1, local copies, waits for them, and re-layouts  0.68 us

profile of v7, /device:TPU:0, one launch (start us, length us, event | category | flops | bytes accessed | tf_op | source)
XLA Modules:
  0.0 15.3 jit_solution(7396840350448889281)
XLA Ops:
  0.0 14.6 %shard_map.28 = f32[3,8,16,128]{3,2,1,0:T(8,128)S(1)} custom-call(f32[3,8,16,128]{3,2,1,0:T(8,128)} %vort_hbm.1, f32[3,8,16,128]{3,2,1,0:T(8,128)} %vel_hbm.1), custom_call_target="tpu_custom_call" | custom-call | tf_op jit(solution)/shard_map/pallas_call | solution.py:467
  14.6 0.7 %copy.4 = f32[3,8,16,128]{3,2,1,0:T(8,128)} copy(f32[3,8,16,128]{3,2,1,0:T(8,128)S(1)} %shard_map.28) | data formatting | bytes 393216
